TPU v7x, 128 devices: a whole 4x4x4 slice. The times are simulated.
128 devices in a mesh: rec: 4 (over z), space: 32 (over y, x, core).
Axes of the slice: x: 4, y: 4, z: 4, core: 2. Of those that a mesh axis runs over, the one named last changes fastest.
Arguments:
- probes: bfloat16 [1048576, 128], P('space'), may hold values from -6 to 6
- band_coeffs: bfloat16 [16, 8, 1048576], P('rec', None, 'space'), may hold values from -2 to 2
- band_offsets: int32 [16, 8], P('rec'), may hold values from -128 to 128, as said below
Outputs:
- q_basis: float32 [1048576, 128], P(('space', 'rec'))
- r_factor: float32 [128, 128], replicated
Inputs may be any that keep to these rules, and one draw needn't show every extreme that they name: `band_offsets`: in every record band 0 has offset -128 and band 1 offset 128.
All inputs are finite; a program needn't handle non-finite values.
Results may differ from a plain program's by a relative error of at most 0.0003.
Values may be sent and summed in bfloat16 or wider, within the bound.
A program may use at most 128 MiB of HBM per device.

v0:
```python
import jax
import jax.numpy as jnp
from jax import lax
from jax.sharding import PartitionSpec as P

HALO = 128


def padded_2(cells, sides, width):
    for axis, dim in sides:
        count = lax.axis_size(axis)
        ends = count - 1
        head = lax.slice_in_dim(cells, 0, width, axis=dim)
        tail = lax.slice_in_dim(cells, cells.shape[dim] - width, cells.shape[dim], axis=dim)
        cells = jnp.concatenate(
            [
                lax.ppermute(tail, axis, [(i, (i + 1) % count) for i in range(ends)]),
                cells,
                lax.ppermute(head, axis, [((i + 1) % count, i) for i in range(ends)]),
            ],
            axis=dim,
        )
    return cells


def accumulate(padded, coeffs, offsets, row_start, count, margin):
    width = padded.shape[1]
    total = jnp.zeros((count, width), jnp.float32)
    for record in range(coeffs.shape[0]):
        for band in range(coeffs.shape[1]):
            offset = offsets[record, band]
            piece = lax.dynamic_slice_in_dim(padded, row_start + margin + offset, count, 0)
            coeff = coeffs[record, band]
            total = total + coeff.astype(jnp.float32)[:, None] * piece.astype(jnp.float32)
    return total


def local(probes, band_coeffs, band_offsets):
    rows = probes.shape[0]
    margin = HALO
    padded = padded_2(probes, (("space", 0),), margin)
    share = rows // lax.axis_size("rec")
    sketch = lax.psum_scatter(
        accumulate(
            padded, band_coeffs, band_offsets, jnp.int32(0), lax.axis_size("rec") * share, margin
        ),
        "rec",
        scatter_dimension=0,
        tiled=True,
    )
    local_gram = jnp.dot(
        sketch.T, sketch, precision=lax.Precision.HIGHEST, preferred_element_type=jnp.float32
    )
    gram = lax.psum(local_gram, ("rec", "space"))
    upper = jnp.linalg.cholesky(gram).T
    scale = jnp.sqrt(jnp.float32(rows * lax.axis_size("space")))
    solved = jax.scipy.linalg.solve_triangular(upper.T, sketch.T, lower=True)
    return (solved.T * scale, upper / scale)


def solution(mesh):
    in_specs = (P("space", None), P("rec", None, "space"), P("rec", None))
    out_specs = (P(("space", "rec"), None), P())
    return jax.shard_map(local, mesh=mesh, in_specs=in_specs, out_specs=out_specs, check_vma=False)
```

profile of v0, /device:TPU:1, one launch (start us, length us, event | category | flops | bytes accessed | tf_op | source)
XLA Modules:
  0.0 890.0 jit_solution(6260652256925387998)
XLA Ops:
  7.2 0.0 reduce-scatter.2.cloned.1.call-start
  7.2 1.4 fusion.2
  8.6 3.3 collective-permute-start.1
  11.9 3.1 collective-permute-start
  15.0 5.8 slice_convert_fusion.30
  20.8 6.8 slice_convert_fusion.31
  27.6 2.1 fusion.3
  29.7 1.9 fusion.4
  71.7 0.8 constant_dynamic-update-slice_fusion.2
  72.6 4.5 constant_dynamic-update-slice_fusion.1
  77.1 0.8 constant_dynamic-update-slice_fusion
  77.9 473.0 %multiply_add_fusion = f32[32768,128]{1,0:T(8,128)} fusion(bf16[33024,128]{1,0:T(8,128)(2,1)S(1)} %constant_dynamic-update-slice_fusion, s32[]{:T(128)S(6)} %select_n.131, f32[32768]{0:T(1024)S(1)} %bitcast.140, s32[]{:T(128)S(6)} %select_n.130, f32[32768]{0:T(1024)S(1)} %bitcast.141, s32[]{:T(128)S(6)} %select_n.129, f32[32768]{0:T(1024)S(1)} %bitcast.111, ...), kind=kLoop, calls=%fused_computation | loop fusion | flops 398458880 | bytes 289407104 | tf_op jit(solution)/shard_map/add | solution.py:34
  550.9 0.2 all-reduce.2.cloned.1.call-start
  551.1 151.7 %reduce-scatter.2.cloned.1.call-done = f32[8192,128]{1,0:T(8,128)} async-done(((f32[32768,128]{1,0:T(8,128)}), f32[8192,128]{1,0:T(8,128)}) %reduce-scatter.2.cloned.1.call-update) | async-done | bytes 4194320 | tf_op jit(solution)/shard_map/reduce_scatter | solution.py:43
  702.8 10.8 %fusion.5 = f32[128,128]{0,1:T(8,128)} fusion(f32[8192,128]{1,0:T(8,128)} %reduce-scatter.2.cloned.1.call-done), kind=kOutput, calls=%fused_computation.50 | convolution fusion | flops 1610612736 | bytes 4259840 | tf_op jit(solution)/shard_map/dot_general | solution.py:51
  713.6 137.4 %all-reduce.2.cloned.1.call-done = f32[128,128]{0,1:T(8,128)} async-done(((f32[128,128]{0,1:T(8,128)}), f32[128,128]{0,1:T(8,128)}) %all-reduce.2.cloned.1.call-update) | async-done | bytes 65552 | tf_op jit(solution)/shard_map/psum | solution.py:54
  851.1 0.9 copy.6
  852.0 0.9 fusion.1
  852.9 11.7 %cholesky.16 = f32[128,128]{1,0:T(8,128)S(1)} custom-call(f32[128,128]{1,0:T(8,128)S(1)} %fusion.1), custom_call_target="Cholesky" | custom-call | tf_op jit(solution)/shard_map/jit(cholesky)/cholesky | solution.py:55
  864.6 0.6 compare_reduce_fusion
  865.3 0.7 multiply_bitcast_fusion
  865.9 0.7 copy.7
  866.7 10.0 %custom-call.7 = f32[1,128,128]{1,2,0:T(8,128)S(1)} custom-call(f32[1,128,128]{2,1,0:T(8,128)S(1)} %get-tuple-element.39), custom_call_target="InvertDiagBlocksLowerTriangular" | custom-call | tf_op jit(solution)/shard_map/jit(_solve_triangular)/triangular_solve | solution.py:57
  876.7 6.5 convolution_multiply_fusion
  (15 shorter events, 0.1 us)
Async XLA Ops:
  7.2 695.6 %reduce-scatter.2.cloned.1.call-start = ((), (), s32[]{:S(2)}) async-start(), calls=%async_computation.1 | async-start | bytes 20971520 | tf_op jit(solution)/shard_map/reduce_scatter | solution.py:43
  8.6 68.5 %collective-permute-start.1 = (bf16[128,128]{1,0:T(8,128)(2,1)}, bf16[128,128]{1,0:T(8,128)(2,1)}, u32[]{:S(2)}, u32[]{:S(2)}) collective-permute-start(bf16[128,128]{1,0:T(8,128)(2,1)} %get-tuple-element.4), channel_id=1, source_target_pairs={{1,0},{2,1},{3,2},{4,3},{5,4},{6,5},{7,6},{8,7},{9,8},{10,9},{11,1... | collective-permute-start | bytes 98312 | tf_op jit(solution)/shard_map/ppermute | solution.py:19
  11.9 59.8 %collective-permute-start = (bf16[128,128]{1,0:T(8,128)(2,1)}, bf16[128,128]{1,0:T(8,128)(2,1)}, u32[]{:S(2)}, u32[]{:S(2)}) collective-permute-start(bf16[128,128]{1,0:T(8,128)(2,1)} %get-tuple-element.5), channel_id=1, source_target_pairs={{0,1},{1,2},{2,3},{3,4},{4,5},{5,6},{6,7},{7,8},{8,9},{9,10},{10,1... | collective-permute-start | bytes 98312 | tf_op jit(solution)/shard_map/ppermute | solution.py:17
  71.7 6.2 copy-start
  71.7 6.2 copy-start.1
  71.7 6.2 copy-start.2
  71.7 6.2 copy-start.3
  71.7 6.2 copy-start.4
  550.9 300.2 %all-reduce.2.cloned.1.call-start = ((), (), s32[]{:S(2)}) async-start(), calls=%async_computation.2 | async-start | bytes 131072 | tf_op jit(solution)/shard_map/psum | solution.py:54
Sparse Core Ops, SparseCore 0:
  551.0 151.7 reduce-scatter.1
  713.8 137.2 all-reduce.1
where the time goes:
time: 891 us; the launch traced here: 890 us
  other arithmetic  509 us (57%)
  waiting for transfers between devices  289 us (32%)
  between operations  54.3 us (6%)
  matrix products  17.3 us (2%)
  local copies, waits for them, and re-layouts  13.1 us (1%)
    add x1, other arithmetic, accumulate(): total + coeff.astype(jnp.float32)[:, None] * piece.astype(jnp.float32)  473 us
    reduce_scatter x1, waiting for transfers between devices, local(): lax.psum_scatter(accumulate(padded, band_coeffs, band_offsets, jnp.int32(...  152 us
    psum x1, waiting for transfers between devices, local(): gram = lax.psum(local_gram, ('rec', 'space'))  137 us
  transfers between devices with their start and end apart: 4, of which 2 were waited for; matrix products, arithmetic and copies ran while one was open for 2% of the time, Pallas kernels for 0%

commit v1 on v0

--- a/solution.py
+++ b/solution.py
@@ -51,7 +51,7 @@
     local_gram = jnp.dot(
         sketch.T, sketch, precision=lax.Precision.HIGHEST, preferred_element_type=jnp.float32
     )
-    gram = lax.psum(local_gram, ("rec", "space"))
+    gram = lax.psum(lax.psum(local_gram, "rec"), "space")
     upper = jnp.linalg.cholesky(gram).T
     scale = jnp.sqrt(jnp.float32(rows * lax.axis_size("space")))
     solved = jax.scipy.linalg.solve_triangular(upper.T, sketch.T, lower=True)

time: 891 us -> 894 us (level)
    psum x1 -> x2, waiting for transfers between devices: 137 us -> 140 us  [local(): gram = lax.psum(lax.psum(local_gram, 'rec'), 'space')]
  transfers between devices with their start and end apart: 4 -> 5, of which waited for: 2 -> 3; matrix products, arithmetic and copies ran while one was open for 2% -> 2% of each run, Pallas kernels for 0% -> 0%
where the time goes in v1:
time: 894 us; the launch traced here: 892 us
  other arithmetic  510 us (57%)
  waiting for transfers between devices  291 us (33%)
  between operations  54 us (6%)
  matrix products  17.3 us (2%)
  local copies, waits for them, and re-layouts  13.1 us (1%)
    add x1, other arithmetic, accumulate(): total + coeff.astype(jnp.float32)[:, None] * piece.astype(jnp.float32)  473 us
    reduce_scatter x1, waiting for transfers between devices, local(): lax.psum_scatter(accumulate(padded, band_coeffs, band_offsets, jnp.int32(...  152 us
    psum x2, waiting for transfers between devices, local(): gram = lax.psum(lax.psum(local_gram, 'rec'), 'space')  140 us
  transfers between devices with their start and end apart: 5, of which 3 were waited for; matrix products, arithmetic and copies ran while one was open for 2% of the time, Pallas kernels for 0%

profile of v1, /device:TPU:1, one launch (start us, length us, event | category | flops | bytes accessed | tf_op | source)
XLA Modules:
  0.0 892.5 jit_solution(8595694422490579808)
XLA Ops:
  7.2 1.4 fusion.2
  8.6 3.3 collective-permute-start.1
  11.9 3.1 collective-permute-start
  15.0 5.8 slice_convert_fusion.30
  20.8 7.2 slice_convert_fusion.31
  28.0 2.1 fusion.3
  30.1 1.9 fusion.4
  72.1 0.8 constant_dynamic-update-slice_fusion.2
  73.0 4.5 constant_dynamic-update-slice_fusion.1
  77.5 0.8 constant_dynamic-update-slice_fusion
  78.3 473.0 %multiply_add_fusion = f32[32768,128]{1,0:T(8,128)} fusion(bf16[33024,128]{1,0:T(8,128)(2,1)S(1)} %constant_dynamic-update-slice_fusion, s32[]{:T(128)S(6)} %select_n.131, f32[32768]{0:T(1024)S(1)} %bitcast.140, s32[]{:T(128)S(6)} %select_n.130, f32[32768]{0:T(1024)S(1)} %bitcast.141, s32[]{:T(128)S(6)} %select_n.129, f32[32768]{0:T(1024)S(1)} %bitcast.111, ...), kind=kLoop, calls=%fused_computation | loop fusion | flops 398458880 | bytes 289407104 | tf_op jit(solution)/shard_map/add | solution.py:34
  551.5 151.7 %reduce-scatter.2.cloned.1.call-done = f32[8192,128]{1,0:T(8,128)} async-done(((f32[32768,128]{1,0:T(8,128)}), f32[8192,128]{1,0:T(8,128)}) %reduce-scatter.2.cloned.1.call-update) | async-done | bytes 4194320 | tf_op jit(solution)/shard_map/reduce_scatter | solution.py:43
  703.2 10.8 %fusion.5 = f32[128,128]{0,1:T(8,128)} fusion(f32[8192,128]{1,0:T(8,128)} %reduce-scatter.2.cloned.1.call-done), kind=kOutput, calls=%fused_computation.50 | convolution fusion | flops 1610612736 | bytes 4259840 | tf_op jit(solution)/shard_map/dot_general | solution.py:51
  714.0 0.3 all-reduce.5.cloned.1.call-start
  714.3 38.5 %all-reduce.3.cloned.1.call-done = f32[128,128]{0,1:T(8,128)} async-done(((f32[128,128]{0,1:T(8,128)}), f32[128,128]{0,1:T(8,128)}) %all-reduce.3.cloned.1.call-update) | async-done | bytes 65552 | tf_op jit(solution)/shard_map/psum | solution.py:54
  752.8 101.2 %all-reduce.5.cloned.1.call-done = f32[128,128]{0,1:T(8,128)} async-done(((f32[128,128]{0,1:T(8,128)}), f32[128,128]{0,1:T(8,128)}) %all-reduce.5.cloned.1.call-update) | async-done | bytes 65552 | tf_op jit(solution)/shard_map/psum | solution.py:54
  854.0 0.9 copy.6
  855.0 0.9 fusion.1
  855.8 11.7 %cholesky.16 = f32[128,128]{1,0:T(8,128)S(1)} custom-call(f32[128,128]{1,0:T(8,128)S(1)} %fusion.1), custom_call_target="Cholesky" | custom-call | tf_op jit(solution)/shard_map/jit(cholesky)/cholesky | solution.py:55
  867.6 0.6 compare_reduce_fusion
  868.2 0.7 multiply_bitcast_fusion
  868.9 0.7 copy.7
  869.6 9.8 %custom-call.7 = f32[1,128,128]{1,2,0:T(8,128)S(1)} custom-call(f32[1,128,128]{2,1,0:T(8,128)S(1)} %get-tuple-element.39), custom_call_target="InvertDiagBlocksLowerTriangular" | custom-call | tf_op jit(solution)/shard_map/jit(_solve_triangular)/triangular_solve | solution.py:57
  879.4 6.5 convolution_multiply_fusion
  (18 shorter events, 0.4 us)
Async XLA Ops:
  7.2 696.0 %reduce-scatter.2.cloned.1.call-start = ((), (), s32[]{:S(2)}) async-start(), calls=%async_computation.1 | async-start | bytes 20971520 | tf_op jit(solution)/shard_map/reduce_scatter | solution.py:43
  8.6 68.9 %collective-permute-start.1 = (bf16[128,128]{1,0:T(8,128)(2,1)}, bf16[128,128]{1,0:T(8,128)(2,1)}, u32[]{:S(2)}, u32[]{:S(2)}) collective-permute-start(bf16[128,128]{1,0:T(8,128)(2,1)} %get-tuple-element.4), channel_id=1, source_target_pairs={{1,0},{2,1},{3,2},{4,3},{5,4},{6,5},{7,6},{8,7},{9,8},{10,9},{11,1... | collective-permute-start | bytes 98312 | tf_op jit(solution)/shard_map/ppermute | solution.py:19
  11.9 60.2 %collective-permute-start = (bf16[128,128]{1,0:T(8,128)(2,1)}, bf16[128,128]{1,0:T(8,128)(2,1)}, u32[]{:S(2)}, u32[]{:S(2)}) collective-permute-start(bf16[128,128]{1,0:T(8,128)(2,1)} %get-tuple-element.5), channel_id=1, source_target_pairs={{0,1},{1,2},{2,3},{3,4},{4,5},{5,6},{6,7},{7,8},{8,9},{9,10},{10,1... | collective-permute-start | bytes 98312 | tf_op jit(solution)/shard_map/ppermute | solution.py:17
  72.1 6.2 copy-start
  72.1 6.2 copy-start.1
  72.1 6.2 copy-start.2
  72.1 6.2 copy-start.3
  72.1 6.2 copy-start.4
  551.3 201.5 %all-reduce.3.cloned.1.call-start = ((), (), s32[]{:S(2)}) async-start(), calls=%async_computation.2 | async-start | bytes 131072 | tf_op jit(solution)/shard_map/psum | solution.py:54
  714.0 140.0 %all-reduce.5.cloned.1.call-start = ((), (), s32[]{:S(2)}) async-start(), calls=%async_computation.3 | async-start | bytes 131072 | tf_op jit(solution)/shard_map/psum | solution.py:54
Sparse Core Ops, SparseCore 0:
  551.4 151.7 reduce-scatter.1
  714.1 38.6 all-reduce.2
  756.1 97.9 all-reduce.4

commit v2 on v0

--- a/solution.py
+++ b/solution.py
@@ -51,7 +51,7 @@
     local_gram = jnp.dot(
         sketch.T, sketch, precision=lax.Precision.HIGHEST, preferred_element_type=jnp.float32
     )
-    gram = lax.psum(local_gram, ("rec", "space"))
+    gram = jnp.sum(lax.all_gather(local_gram, ("rec", "space")), axis=0)
     upper = jnp.linalg.cholesky(gram).T
     scale = jnp.sqrt(jnp.float32(rows * lax.axis_size("space")))
     solved = jax.scipy.linalg.solve_triangular(upper.T, sketch.T, lower=True)

time: 891 us -> 826 us (0.927)
  waiting for transfers between devices: 289 us -> 222 us
    psum x1 -> x0, waiting for transfers between devices: 137 us -> none  [local(): gram = lax.psum(local_gram, ('rec', 'space'))]
    all_gather x0 -> x1, waiting for transfers between devices: none -> 70.2 us  [local(): gram = jnp.sum(lax.all_gather(local_gram, ('rec', 'space')), axis=0)]
  transfers between devices with their start and end apart: 4 -> 4, of which waited for: 2 -> 2; matrix products, arithmetic and copies ran while one was open for 2% -> 3% of each run, Pallas kernels for 0% -> 0%
where the time goes in v2:
time: 826 us; the launch traced here: 825 us
  other arithmetic  512 us (62%)
  waiting for transfers between devices  222 us (27%)
  between operations  54.3 us (7%)
  matrix products  17.3 us (2%)
  local copies, waits for them, and re-layouts  12.3 us (1%)
    add x1, other arithmetic, accumulate(): total + coeff.astype(jnp.float32)[:, None] * piece.astype(jnp.float32)  473 us
    reduce_scatter x1, waiting for transfers between devices, local(): lax.psum_scatter(accumulate(padded, band_coeffs, band_offsets, jnp.int32(...  152 us
    all_gather x1, waiting for transfers between devices, local(): gram = jnp.sum(lax.all_gather(local_gram, ('rec', 'space')), axis=0)  70.2 us
  transfers between devices with their start and end apart: 4, of which 2 were waited for; matrix products, arithmetic and copies ran while one was open for 3% of the time, Pallas kernels for 0%

profile of v2, /device:TPU:1, one launch (start us, length us, event | category | flops | bytes accessed | tf_op | source)
XLA Modules:
  0.0 824.9 jit_solution(10657977405792252166)
XLA Ops:
  7.2 0.0 reduce-scatter.2.cloned.1.call-start
  7.2 1.4 fusion.2
  8.6 3.3 collective-permute-start.1
  11.9 3.1 collective-permute-start
  15.0 5.8 slice_convert_fusion.30
  20.8 6.8 slice_convert_fusion.31
  27.6 2.1 fusion.3
  29.7 1.9 fusion.4
  71.7 0.8 constant_dynamic-update-slice_fusion.2
  72.6 4.5 constant_dynamic-update-slice_fusion.1
  77.1 0.8 constant_dynamic-update-slice_fusion
  77.9 473.0 %multiply_add_fusion = f32[32768,128]{1,0:T(8,128)} fusion(bf16[33024,128]{1,0:T(8,128)(2,1)S(1)} %constant_dynamic-update-slice_fusion, s32[]{:T(128)S(6)} %select_n.131, f32[32768]{0:T(1024)S(1)} %bitcast.142, s32[]{:T(128)S(6)} %select_n.130, f32[32768]{0:T(1024)S(1)} %bitcast.143, s32[]{:T(128)S(6)} %select_n.129, f32[32768]{0:T(1024)S(1)} %bitcast.113, ...), kind=kLoop, calls=%fused_computation | loop fusion | flops 398458880 | bytes 289407104 | tf_op jit(solution)/shard_map/add | solution.py:34
  550.9 0.2 all-gather.3.cloned.1.call-start
  551.1 151.7 %reduce-scatter.2.cloned.1.call-done = f32[8192,128]{1,0:T(8,128)} async-done(((f32[32768,128]{1,0:T(8,128)}), f32[8192,128]{1,0:T(8,128)}) %reduce-scatter.2.cloned.1.call-update) | async-done | bytes 4194320 | tf_op jit(solution)/shard_map/reduce_scatter | solution.py:43
  702.8 10.8 %fusion.5 = f32[128,128]{1,0:T(8,128)} fusion(f32[8192,128]{1,0:T(8,128)} %reduce-scatter.2.cloned.1.call-done), kind=kOutput, calls=%fused_computation.50 | convolution fusion | flops 1610612736 | bytes 4259840 | tf_op jit(solution)/shard_map/dot_general | solution.py:51
  713.6 70.2 %all-gather.3.cloned.1.call-done = f32[16384,128]{1,0:T(8,128)} async-done(((f32[128,128]{1,0:T(8,128)}), f32[16384,128]{1,0:T(8,128)}) %all-gather.3.cloned.1.call-update) | async-done | bytes 8388624 | tf_op jit(solution)/shard_map/all_gather | solution.py:54
  783.9 3.8 reduce_sum.9
  787.7 0.1 copy.7
  787.8 11.7 %cholesky.16 = f32[128,128]{1,0:T(8,128)S(1)} custom-call(f32[128,128]{1,0:T(8,128)S(1)} %fusion.1), custom_call_target="Cholesky" | custom-call | tf_op jit(solution)/shard_map/jit(cholesky)/cholesky | solution.py:55
  799.5 0.6 compare_reduce_fusion
  800.2 0.7 multiply_bitcast_fusion
  800.8 0.7 copy.8
  801.6 10.0 %custom-call.7 = f32[1,128,128]{1,2,0:T(8,128)S(1)} custom-call(f32[1,128,128]{2,1,0:T(8,128)S(1)} %get-tuple-element.41), custom_call_target="InvertDiagBlocksLowerTriangular" | custom-call | tf_op jit(solution)/shard_map/jit(_solve_triangular)/triangular_solve | solution.py:57
  811.5 6.5 convolution_multiply_fusion
  (16 shorter events, 0.1 us)
Async XLA Ops:
  7.2 695.6 %reduce-scatter.2.cloned.1.call-start = ((), (), s32[]{:S(2)}) async-start(), calls=%async_computation.1 | async-start | bytes 20971520 | tf_op jit(solution)/shard_map/reduce_scatter | solution.py:43
  8.6 68.5 %collective-permute-start.1 = (bf16[128,128]{1,0:T(8,128)(2,1)}, bf16[128,128]{1,0:T(8,128)(2,1)}, u32[]{:S(2)}, u32[]{:S(2)}) collective-permute-start(bf16[128,128]{1,0:T(8,128)(2,1)} %get-tuple-element.6), channel_id=1, source_target_pairs={{1,0},{2,1},{3,2},{4,3},{5,4},{6,5},{7,6},{8,7},{9,8},{10,9},{11,1... | collective-permute-start | bytes 98312 | tf_op jit(solution)/shard_map/ppermute | solution.py:19
  11.9 59.8 %collective-permute-start = (bf16[128,128]{1,0:T(8,128)(2,1)}, bf16[128,128]{1,0:T(8,128)(2,1)}, u32[]{:S(2)}, u32[]{:S(2)}) collective-permute-start(bf16[128,128]{1,0:T(8,128)(2,1)} %get-tuple-element.7), channel_id=1, source_target_pairs={{0,1},{1,2},{2,3},{3,4},{4,5},{5,6},{6,7},{7,8},{8,9},{9,10},{10,1... | collective-permute-start | bytes 98312 | tf_op jit(solution)/shard_map/ppermute | solution.py:17
  71.7 6.2 copy-start
  71.7 6.2 copy-start.1
  71.7 6.2 copy-start.2
  71.7 6.2 copy-start.3
  71.7 6.2 copy-start.4
  550.9 233.0 %all-gather.3.cloned.1.call-start = ((), (), s32[]{:S(2)}) async-start(), calls=%async_computation.2 | async-start | bytes 8454144 | tf_op jit(solution)/shard_map/all_gather | solution.py:54
Sparse Core Ops, SparseCore 0:
  551.0 151.7 reduce-scatter.1
  713.7 70.0 all-gather.2
